TPU v7x, 128 devices: a whole 4x4x4 slice. The times are simulated.
128 devices in a mesh: row: 8 (over x, core), col: 16 (over z, y).
Axes of the slice: x: 4, y: 4, z: 4, core: 2. Of those that a mesh axis runs over, the one named last changes fastest.
Arguments:
- basis: bfloat16 [1152, 256, 128], P(('row', 'col')), may hold values from -1.5 to 1.5
- row_index: int32 [1152, 128], P(('row', 'col')), may hold values from 0 to 255
- group_slot: int32 [1152], P(('row', 'col')), may hold values from 0 to 1535, as said below
- x_blocks: bfloat16 [96, 256, 256], P('row', 'col')
- zinv_blocks: bfloat16 [96, 256, 256], P('row', 'col')
Outputs:
- schur_tiles: float32 [96, 2048, 2048], P('row', None, 'col')
Inputs may be any that keep to these rules, and one draw needn't show every extreme that they name: Values are distinct; group_slot // 16 is the group's PSD block and group_slot % 16 its position there. A group stored on the device at (row index a, col index c) has its position among c * 1 to c + 1 - 1. Of the groups of one device, at most 2 belong to blocks of one index of row (blocks b with b // 12 equal to it), and every device reaches 2 for some index. The positions that the blocks of one index of row have on one index of col hold exactly 9 groups.
All inputs are finite; a program needn't handle non-finite values.
Results may differ from a plain program's by a relative error of at most 0.00048.
Values may be sent and summed in bfloat16 or wider, within the bound.
A program may use at most 192 MiB of HBM per device.

v0:
```python
import jax
import jax.numpy as jnp
from jax import lax
from jax.sharding import PartitionSpec as P

GMAX = 16


def sent_together(arrays, axis, split_dim, concat_dim, along):
    columns = [a.reshape(*a.shape[:along], -1) for a in arrays]
    both = jnp.concatenate(columns, axis=along)
    result, at, done = (
        lax.all_to_all(both, axis, split_axis=split_dim, concat_axis=concat_dim, tiled=True),
        0,
        [],
    )
    for a, column in zip(arrays, columns):
        slab = result[..., at : at + column.shape[along]]
        done.append(slab.reshape(*slab.shape[:along], *a.shape[along:]))
        at += column.shape[along]
    return tuple(done)


def side_by_side(arrays, axis, dim, along):
    widths = [a.shape[along] for a in arrays]
    both = jnp.concatenate(arrays, axis=along)
    result = lax.all_gather(both, axis, axis=dim, tiled=True)
    return tuple(jnp.split(result, [sum(widths[:k]) for k in range(1, len(widths))], axis=along))


def place_rows(selector, values):
    flat_values = values.reshape(values.shape[0], -1)
    moved_rows = jnp.dot(selector, flat_values, preferred_element_type=jnp.float32)
    return moved_rows.astype(values.dtype).reshape((selector.shape[0],) + values.shape[1:])


def place_ints(selector, values):
    moved_rows = jnp.dot(selector, values, preferred_element_type=jnp.int32)
    return moved_rows


def pair_tiles(members):
    stacked, x_full, z_full, rows_all, mask_all, near_basis, near_rows, near_mask = members
    group_width = near_basis.shape[-1]
    order = x_full.shape[0]
    positions = rows_all.shape[0]
    order_ids = jnp.arange(order, dtype=jnp.int32)
    row_pick = (rows_all.reshape(-1)[:, None] == order_ids[None, :]).astype(jnp.bfloat16)
    x_rows = (
        jnp.dot(row_pick, x_full, preferred_element_type=jnp.float32)
        .astype(jnp.bfloat16)
        .reshape(positions, group_width, order)
    )
    z_rows = (
        jnp.dot(row_pick, z_full, preferred_element_type=jnp.float32)
        .astype(jnp.bfloat16)
        .reshape(positions, group_width, order)
    )
    images = jnp.concatenate([stacked[:, 0], x_rows, stacked[:, 1], z_rows], axis=1)
    products = jnp.einsum("pcn,snk->pcsk", images, near_basis, preferred_element_type=jnp.float32)
    products = products.reshape(products.shape[0], products.shape[1], -1)
    column_pick = (order_ids[:, None] == near_rows.reshape(-1)[None, :]).astype(jnp.bfloat16)
    picked = jnp.einsum("pcn,nk->pck", images, column_pick, preferred_element_type=jnp.float32)
    upper = 2 * group_width
    third = 3 * group_width
    tile_sum = (
        products[:, group_width:upper] * picked[:, upper:third]
        + picked[:, group_width:upper] * products[:, upper:third]
    )
    tile_sum = (
        tile_sum
        + products[:, :group_width] * picked[:, third:]
        + picked[:, :group_width] * products[:, third:]
    )
    row_mask = mask_all.astype(jnp.float32)
    column_mask = jnp.repeat(near_mask.astype(jnp.float32), group_width)
    tile_sum = tile_sum * row_mask[:, None, None] * column_mask[None, None, :]
    return tile_sum.reshape(-1, tile_sum.shape[2])


def body(basis, row_index, group_slot, x_blocks, zinv_blocks):
    row_count = lax.axis_size("row")
    col_count = lax.axis_size("col")
    my_row = lax.axis_index("row")
    my_col = lax.axis_index("col")
    groups = basis.shape[0]
    owned = x_blocks.shape[0]
    places = GMAX // col_count
    capacity = (groups + row_count - 1) // row_count
    slot_count = row_count * capacity
    block_of = group_slot // GMAX
    owner_of = block_of // owned
    same_owner = (owner_of[:, None] == owner_of[None, :]).astype(jnp.int32)
    earlier = jnp.sum(jnp.tril(same_owner, -1), axis=1)
    target = owner_of * capacity + earlier
    choose = target[None, :] == jnp.arange(slot_count, dtype=jnp.int32)[:, None]
    send_basis = place_rows(choose.astype(jnp.bfloat16), basis)
    send_rows = place_ints(choose.astype(jnp.int32), row_index)
    send_slot = place_ints(choose.astype(jnp.int32), (group_slot + 1)[:, None])[:, 0] - 1
    got_basis, got_rows, got_slot = (
        lax.all_to_all(send_basis, "row", split_axis=0, concat_axis=0, tiled=True),
        *sent_together((send_rows, send_slot), "row", 0, 0, 1),
    )
    is_valid = got_slot >= 0
    spot_index = (got_slot // GMAX - my_row * owned) * places + (got_slot % GMAX - my_col * places)
    settle = (
        spot_index[None, :] == jnp.arange(owned * places, dtype=jnp.int32)[:, None]
    ) & is_valid[None, :]
    near_basis = place_rows(settle.astype(jnp.bfloat16), got_basis)
    near_basis = near_basis.reshape((owned, places) + near_basis.shape[1:])
    near_rows = place_ints(settle.astype(jnp.int32), got_rows).reshape(owned, places, -1)
    near_mask = (
        jnp.sum(settle.astype(jnp.float32), axis=1).astype(jnp.bfloat16).reshape(owned, places)
    )
    x_full, z_full, all_basis, rows_all, mask_all = (
        *side_by_side((x_blocks, zinv_blocks), "col", 1, 0),
        lax.all_gather(near_basis, "col", axis=1, tiled=True),
        lax.all_gather(near_rows, "col", axis=1, tiled=True),
        lax.all_gather(near_mask, "col", axis=1, tiled=True),
    )
    all_x = jnp.einsum(
        "jpnc,jnm->jpcm", all_basis, x_full, preferred_element_type=jnp.float32
    ).astype(jnp.bfloat16)
    all_z = jnp.einsum(
        "jpnc,jnm->jpcm", all_basis, z_full, preferred_element_type=jnp.float32
    ).astype(jnp.bfloat16)
    stacked = jnp.stack([all_x, all_z], axis=2)
    tile_blocks = lax.map(
        pair_tiles, (stacked, x_full, z_full, rows_all, mask_all, near_basis, near_rows, near_mask)
    )
    return tile_blocks


def solution(mesh):
    placed = (
        P(("row", "col"), None, None),
        P(("row", "col"), None),
        P(("row", "col")),
        P("row", "col", None),
        P("row", "col", None),
    )
    return jax.shard_map(
        body, mesh=mesh, in_specs=placed, out_specs=P("row", None, "col"), check_vma=False
    )
```

profile of v0, /device:TPU:2, one launch (start us, length us, event | category | flops | bytes accessed | tf_op | source)
XLA Modules:
  0.0 410.7 jit_solution(17968727844061814337)
XLA Ops:
  10.7 4.8 %all-to-all-start = ((s32[8,2,129]{2,1,0:T(2,128)}), s32[8,2,129]{2,1,0:T(2,128)S(1)}, u32[]{:S(2)}, u32[]{:S(2)}) async-start(s32[8,2,129]{2,1,0:T(2,128)} %pad_add_fusion), calls=%async_computation | async-start | bytes 32768 | tf_op jit(solution)/shard_map/all_to_all | solution.py:13
  19.4 4.9 %all-to-all-start.1 = ((bf16[16,256,128]{2,1,0:T(8,128)(2,1)}), bf16[16,256,128]{2,1,0:T(8,128)(2,1)S(1)}, u32[]{:S(2)}, u32[]{:S(2)}) async-start(bf16[16,256,128]{2,1,0:T(8,128)(2,1)} %bitcast.45), calls=%async_computation.1 | async-start | bytes 2097152 | tf_op jit(solution)/shard_map/all_to_all | solution.py:101
  24.5 14.3 %all-to-all-done.1 = bf16[16,256,128]{2,1,0:T(8,128)(2,1)S(1)} async-done(((bf16[16,256,128]{2,1,0:T(8,128)(2,1)}), bf16[16,256,128]{2,1,0:T(8,128)(2,1)S(1)}, u32[]{:S(2)}, u32[]{:S(2)}) %all-to-all-start.1) | async-done | bytes 1048608 | tf_op jit(solution)/shard_map/all_to_all | solution.py:101
  42.5 25.5 %all-gather = s32[12,2048]{1,0:T(8,128)S(1)} all-gather(s32[12,128]{1,0:T(8,128)S(1)} %fusion.32), channel_id=2, replica_groups=mesh['row'=8,'col'=16] {'col'}, dimensions={1}, use_global_device_ids=true | all-gather | bytes 104448 | tf_op jit(solution)/shard_map/all_gather | solution.py:118
  68.1 20.1 %all-gather.1 = bf16[16,1,12]{2,1,0:T(2,128)(2,1)S(1)} all-gather(bf16[1,1,12]{2,1,0:T(2,128)(2,1)S(1)} %bitcast.137), channel_id=1, replica_groups=mesh['row'=8,'col'=16] {'col'}, dimensions={0}, use_global_device_ids=true | all-gather | bytes 408 | tf_op jit(solution)/shard_map/all_gather | solution.py:119
  91.6 64.0 %all-gather.5.cloned.1.call-done = bf16[12,16,256,128]{2,3,1,0:T(8,128)(2,1)} async-done(((bf16[12,1,256,128]{2,3,1,0:T(8,128)(2,1)}), bf16[12,16,256,128]{2,3,1,0:T(8,128)(2,1)}) %all-gather.5.cloned.1.call-update) | async-done | bytes 12582928 | tf_op jit(solution)/shard_map/all_gather | solution.py:117
  155.7 11.4 %convert_bitcast_fusion = bf16[12,16,1,128,256]{4,3,1,0,2:T(8,128)(2,1)} fusion(bf16[12,16,256,128]{2,3,1,0:T(8,128)(2,1)} %all-gather.5.cloned.1.call-done, bf16[24,256,256]{2,1,0:T(8,128)(2,1)} %all-gather.7.cloned.1.call-done), kind=kOutput, calls=%fused_computation.45 | convolution fusion | flops 3227516928 | bytes 26738688 | tf_op jit(solution)/shard_map/jpnc,jnm->jpcm/dot_general | solution.py:124
  168.7 7.7 %convert_bitcast_fusion.1 = bf16[12,16,1,128,256]{4,3,1,0,2:T(8,128)(2,1)} fusion(bf16[12,16,256,128]{2,3,1,0:T(8,128)(2,1)S(1)} %copy-done.2, bf16[24,256,256]{2,1,0:T(8,128)(2,1)} %all-gather.7.cloned.1.call-done), kind=kOutput, calls=%fused_computation.46 | convolution fusion | flops 3227516928 | bytes 26738688 | tf_op jit(solution)/shard_map/jpnc,jnm->jpcm/dot_general | solution.py:121
  176.4 20.5 %pad_maximum_fusion.3 = bf16[12,16,2,128,256]{4,3,1,0,2:T(8,128)(2,1)} fusion(bf16[12,16,1,128,256]{4,3,1,0,2:T(8,128)(2,1)} %convert_bitcast_fusion, bf16[12,16,1,128,256]{4,3,1,0,2:T(8,128)(2,1)} %convert_bitcast_fusion.1), kind=kLoop, calls=%fused_computation.44 | loop fusion | flops 12582912 | bytes 50331648 | tf_op jit(solution)/shard_map/stack | solution.py:127
  197.0 206.1 %while.10 = (s32[]{:T(128)}, f32[12,2048,128]{2,1,0:T(8,128)}, bf16[12,16,2,128,256]{4,3,1,0,2:T(8,128)(2,1)}, s32[12,16,128]{2,1,0:T(8,128)S(1)}, bf16[12,256,2...) while((s32[]{:T(128)}, f32[12,2048,128]{2,1,0:T(8,128)}, ...), condition=%wide.region_3.4_spmd, body=%wide.region_2.3_spmd.sunk | while | flops 1648656384 | bytes 39161136 | solution.py:128
  204.0 3.6 fusion.70
  208.7 4.4 %fusion.74 = f32[16,128,128]{2,1,0:T(8,128)S(1)} fusion(f32[16,512,128]{2,1,0:T(8,128)} %fusion.70, f32[16,512,128]{2,1,0:T(8,128)} %fusion.72, f32[]{:T(128)S(6)} %convert.11, f32[16]{0:T(128)S(1)} %fusion.73), kind=kLoop, calls=%fused_computation.8.clone.1 | loop fusion | flops 2359296 | bytes 9437252 | tf_op jit(solution)/shard_map/while/body/eval_jaxpr/mul | solution.py:77
  225.9 4.4 %fusion.74 = f32[16,128,128]{2,1,0:T(8,128)S(1)} fusion(f32[16,512,128]{2,1,0:T(8,128)} %fusion.70, f32[16,512,128]{2,1,0:T(8,128)} %fusion.72, f32[]{:T(128)S(6)} %convert.11, f32[16]{0:T(128)S(1)} %fusion.73), kind=kLoop, calls=%fused_computation.8.clone.1 | loop fusion | flops 2359296 | bytes 9437252 | tf_op jit(solution)/shard_map/while/body/eval_jaxpr/mul | solution.py:77
  243.1 4.4 %fusion.74 = f32[16,128,128]{2,1,0:T(8,128)S(1)} fusion(f32[16,512,128]{2,1,0:T(8,128)} %fusion.70, f32[16,512,128]{2,1,0:T(8,128)} %fusion.72, f32[]{:T(128)S(6)} %convert.11, f32[16]{0:T(128)S(1)} %fusion.73), kind=kLoop, calls=%fused_computation.8.clone.1 | loop fusion | flops 2359296 | bytes 9437252 | tf_op jit(solution)/shard_map/while/body/eval_jaxpr/mul | solution.py:77
  255.6 3.6 fusion.70
  260.3 4.4 %fusion.74 = f32[16,128,128]{2,1,0:T(8,128)S(1)} fusion(f32[16,512,128]{2,1,0:T(8,128)} %fusion.70, f32[16,512,128]{2,1,0:T(8,128)} %fusion.72, f32[]{:T(128)S(6)} %convert.11, f32[16]{0:T(128)S(1)} %fusion.73), kind=kLoop, calls=%fused_computation.8.clone.1 | loop fusion | flops 2359296 | bytes 9437252 | tf_op jit(solution)/shard_map/while/body/eval_jaxpr/mul | solution.py:77
  277.5 4.4 %fusion.74 = f32[16,128,128]{2,1,0:T(8,128)S(1)} fusion(f32[16,512,128]{2,1,0:T(8,128)} %fusion.70, f32[16,512,128]{2,1,0:T(8,128)} %fusion.72, f32[]{:T(128)S(6)} %convert.11, f32[16]{0:T(128)S(1)} %fusion.73), kind=kLoop, calls=%fused_computation.8.clone.1 | loop fusion | flops 2359296 | bytes 9437252 | tf_op jit(solution)/shard_map/while/body/eval_jaxpr/mul | solution.py:77
  294.6 4.4 %fusion.74 = f32[16,128,128]{2,1,0:T(8,128)S(1)} fusion(f32[16,512,128]{2,1,0:T(8,128)} %fusion.70, f32[16,512,128]{2,1,0:T(8,128)} %fusion.72, f32[]{:T(128)S(6)} %convert.11, f32[16]{0:T(128)S(1)} %fusion.73), kind=kLoop, calls=%fused_computation.8.clone.1 | loop fusion | flops 2359296 | bytes 9437252 | tf_op jit(solution)/shard_map/while/body/eval_jaxpr/mul | solution.py:77
  311.8 4.4 %fusion.74 = f32[16,128,128]{2,1,0:T(8,128)S(1)} fusion(f32[16,512,128]{2,1,0:T(8,128)} %fusion.70, f32[16,512,128]{2,1,0:T(8,128)} %fusion.72, f32[]{:T(128)S(6)} %convert.11, f32[16]{0:T(128)S(1)} %fusion.73), kind=kLoop, calls=%fused_computation.8.clone.1 | loop fusion | flops 2359296 | bytes 9437252 | tf_op jit(solution)/shard_map/while/body/eval_jaxpr/mul | solution.py:77
  329.0 4.4 %fusion.74 = f32[16,128,128]{2,1,0:T(8,128)S(1)} fusion(f32[16,512,128]{2,1,0:T(8,128)} %fusion.70, f32[16,512,128]{2,1,0:T(8,128)} %fusion.72, f32[]{:T(128)S(6)} %convert.11, f32[16]{0:T(128)S(1)} %fusion.73), kind=kLoop, calls=%fused_computation.8.clone.1 | loop fusion | flops 2359296 | bytes 9437252 | tf_op jit(solution)/shard_map/while/body/eval_jaxpr/mul | solution.py:77
  346.2 4.4 %fusion.74 = f32[16,128,128]{2,1,0:T(8,128)S(1)} fusion(f32[16,512,128]{2,1,0:T(8,128)} %fusion.70, f32[16,512,128]{2,1,0:T(8,128)} %fusion.72, f32[]{:T(128)S(6)} %convert.11, f32[16]{0:T(128)S(1)} %fusion.73), kind=kLoop, calls=%fused_computation.8.clone.1 | loop fusion | flops 2359296 | bytes 9437252 | tf_op jit(solution)/shard_map/while/body/eval_jaxpr/mul | solution.py:77
  363.3 4.4 %fusion.74 = f32[16,128,128]{2,1,0:T(8,128)S(1)} fusion(f32[16,512,128]{2,1,0:T(8,128)} %fusion.70, f32[16,512,128]{2,1,0:T(8,128)} %fusion.72, f32[]{:T(128)S(6)} %convert.11, f32[16]{0:T(128)S(1)} %fusion.73), kind=kLoop, calls=%fused_computation.8.clone.1 | loop fusion | flops 2359296 | bytes 9437252 | tf_op jit(solution)/shard_map/while/body/eval_jaxpr/mul | solution.py:77
  380.5 4.4 %fusion.74 = f32[16,128,128]{2,1,0:T(8,128)S(1)} fusion(f32[16,512,128]{2,1,0:T(8,128)} %fusion.70, f32[16,512,128]{2,1,0:T(8,128)} %fusion.72, f32[]{:T(128)S(6)} %convert.11, f32[16]{0:T(128)S(1)} %fusion.73), kind=kLoop, calls=%fused_computation.8.clone.1 | loop fusion | flops 2359296 | bytes 9437252 | tf_op jit(solution)/shard_map/while/body/eval_jaxpr/mul | solution.py:77
  397.7 4.4 %fusion.74 = f32[16,128,128]{2,1,0:T(8,128)S(1)} fusion(f32[16,512,128]{2,1,0:T(8,128)} %fusion.70, f32[16,512,128]{2,1,0:T(8,128)} %fusion.72, f32[]{:T(128)S(6)} %convert.11, f32[16]{0:T(128)S(1)} %fusion.73), kind=kLoop, calls=%fused_computation.8.clone.1 | loop fusion | flops 2359296 | bytes 9437252 | tf_op jit(solution)/shard_map/while/body/eval_jaxpr/mul | solution.py:77
  (169 shorter events, 157.0 us)
Async XLA Ops:
  6.5 3.4 copy-start
  6.5 81.8 %all-gather.7.cloned.1.call-start = ((), (), s32[]{:S(2)}) async-start(), calls=%async_computation.3 | async-start | bytes 3342336 | tf_op jit(solution)/shard_map/all_gather | solution.py:27
  10.7 8.7 %all-to-all-start = ((s32[8,2,129]{2,1,0:T(2,128)}), s32[8,2,129]{2,1,0:T(2,128)S(1)}, u32[]{:S(2)}, u32[]{:S(2)}) async-start(s32[8,2,129]{2,1,0:T(2,128)} %pad_add_fusion), calls=%async_computation | async-start | bytes 32768 | tf_op jit(solution)/shard_map/all_to_all | solution.py:13
  19.4 19.4 %all-to-all-start.1 = ((bf16[16,256,128]{2,1,0:T(8,128)(2,1)}), bf16[16,256,128]{2,1,0:T(8,128)(2,1)S(1)}, u32[]{:S(2)}, u32[]{:S(2)}) async-start(bf16[16,256,128]{2,1,0:T(8,128)(2,1)} %bitcast.45), calls=%async_computation.1 | async-start | bytes 2097152 | tf_op jit(solution)/shard_map/all_to_all | solution.py:101
  24.4 131.3 %all-gather.5.cloned.1.call-start = ((), (), s32[]{:S(2)}) async-start(), calls=%async_computation.2 | async-start | bytes 13369344 | tf_op jit(solution)/shard_map/all_gather | solution.py:117
  155.7 13.0 %copy-start.2 = (bf16[12,16,256,128]{2,3,1,0:T(8,128)(2,1)S(1)}, bf16[12,16,256,128]{2,3,1,0:T(8,128)(2,1)}, u32[]{:S(2)}) copy-start(bf16[12,16,256,128]{2,3,1,0:T(8,128)(2,1)} %all-gather.5.cloned.1.call-done) | copy-start | bytes 37748740
  403.1 0.7 copy-start.1
Sparse Core Ops, SparseCore 0:
  9.4 54.4 all-gather.6
  66.1 89.5 all-gather.4
where the time goes:
time: 413 us; the launch traced here: 411 us
  matrix products  126 us (31%)
  waiting for transfers between devices  78.9 us (19%)
  other arithmetic  76.2 us (18%)
  local copies, waits for them, and re-layouts  53.5 us (13%)
  blocking collectives  45.6 us (11%)
  between operations  13.5 us (3%)
  starting transfers between devices  9.77 us (2%)
  loops' own time  7.33 us (2%)
    all_gather x1, waiting for transfers between devices, body(): lax.all_gather(near_basis, 'col', axis=1, tiled=True)  64 us
    mul x12, other arithmetic, pair_tiles(): tile_sum = tile_sum * row_mask[:, None, None] * column_mask[None, None, :]  52.3 us
    dot_general x12, matrix products, pair_tiles(): jnp.einsum('pcn,snk->pcsk', images, near_basis, preferred_element_type=jn...  43 us
    dot_general x12, matrix products, pair_tiles(): jnp.einsum('pcn,nk->pck', images, column_pick, preferred_element_type=jnp...  32.7 us
    all_gather x1, blocking collectives, body(): lax.all_gather(near_rows, 'col', axis=1, tiled=True)  25.5 us
    squeeze x12, local copies, waits for them, and re-layouts, body(): lax.map(pair_tiles, (stacked, x_full, z_full, rows_all, mask_all, near_ba...  20.8 us
    another operation x1, other arithmetic, body(): stacked = jnp.stack([all_x, all_z], axis=2)  20.5 us
    all_gather x1, blocking collectives, body(): lax.all_gather(near_mask, 'col', axis=1, tiled=True)  20.1 us
  transfers between devices with their start and end apart: 4, of which 3 were waited for; matrix products, arithmetic and copies ran while one was open for 3% of the time, Pallas kernels for 0%

commit v1 on v0

v1 whole, which is shorter than its diff:
```python
import jax
import jax.numpy as jnp
from jax import lax
from jax.experimental import pallas as pl
from jax.experimental.pallas import tpu as pltpu
from jax.sharding import PartitionSpec as P

bf16, f32, i32 = jnp.bfloat16, jnp.float32, jnp.int32
N, C, GMAX = 256, 128, 16
ROWS, COLS, SIDE = 8, 16, 4
OWNED, GROUPS, PAIR = 12, 9, 2
SLAB = N // COLS
CLASS_ROWS = C // 2
HALF_ROWS = CLASS_ROWS // 2
WHOLE = None
BATCHES = (
    ((0, 0), (1, 0), (3, 0), (0, 1)),
    ((0, 3), (2, 0), (0, 2), (1, 1)),
    ((1, 3), (3, 1), (3, 3)),
    ((2, 1), (1, 2)),
    ((2, 3), (3, 2), (2, 2)),
)
UNROLL = 3


def col_of(y, z):
    return z * SIDE + y


def one_hot_rows(rows):
    column = jnp.broadcast_to(rows, (C, C)).T
    lanes = lax.broadcasted_iota(i32, (C, C), 1)
    both = jnp.concatenate([column == lanes, column == lanes + C], axis=1)
    return jnp.where(both, 1.0, 0.0).astype(bf16)


def row_at(table, at):
    down = lax.broadcasted_iota(i32, table.shape, 0)
    return jnp.sum(jnp.where(down == at, table, 0), axis=0, keepdims=True)


def tiles_of(parts, x, z, q):
    stack = jnp.concatenate([a for ut, rows in parts for a in (ut, one_hot_rows(rows))], axis=0)
    sx = jnp.dot(stack, x, preferred_element_type=f32).astype(bf16)
    sz = jnp.dot(stack, z, preferred_element_type=f32).astype(bf16)
    tx = jnp.dot(sx, q, preferred_element_type=f32)
    tz = jnp.dot(sz, q, preferred_element_type=f32)
    out = []
    for i in range(len(parts)):
        lo, mid, hi = 2 * C * i, 2 * C * i + C, 2 * C * i + 2 * C
        su0, se0, su1, se1 = tx[lo:mid, :C], tx[lo:mid, C:], tx[mid:hi, :C], tx[mid:hi, C:]
        su2, se2, su3, se3 = tz[lo:mid, :C], tz[lo:mid, C:], tz[mid:hi, :C], tz[mid:hi, C:]
        out.append(su1 * se2 + se1 * su2 + su0 * se3 + se0 * su3)
    return out


def gather_kernel(
    slot_ref, basis_ref, rows_ref, x_ref, z_ref, tiles_ref, block_ref,
    send_ut, got_ut, send_meta, got_meta, all_meta, small_got, small_all,
    x_full, z_full, q_all, *rest,
):
    u_bufs = rest[:16]
    (xz_send, xz_recv, u_send, u_recv, a_send, a_recv, m_send, m_recv, b_send, b_recv, local) = rest[16:]
    my_row, my_col = lax.axis_index("row"), lax.axis_index("col")
    my_y, my_z = lax.rem(my_col, SIDE), my_col // SIDE

    row_peers = [lax.rem(my_row + d, ROWS) for d in range(1, ROWS)]
    col_peers = [lax.rem(my_col + d, COLS) for d in range(1, COLS)]
    barrier = pltpu.get_barrier_semaphore()
    for r in row_peers:
        pl.semaphore_signal(barrier, inc=1, device_id={"row": r})
    for c in col_peers:
        pl.semaphore_signal(barrier, inc=1, device_id={"col": c})

    def source_col(oy, oz):
        return col_of(lax.rem(my_y + SIDE - oy, SIDE), lax.rem(my_z + SIDE - oz, SIDE))

    def yz(cls, off):
        return off if cls == 0 else (off[1], off[0])

    def moved(off, dim, sign):
        new = list(off)
        new[dim] = (new[dim] + sign) % SIDE
        return tuple(new)

    def neighbour(cls, dim, sign):
        along_y = (dim == 0) == (cls == 0)
        y = lax.rem(my_y + SIDE + sign, SIDE) if along_y else my_y
        z = my_z if along_y else lax.rem(my_z + SIDE + sign, SIDE)
        return {"col": col_of(y, z)}

    def sem_at(cls, off, half):
        return cls * 32 + (off[0] * SIDE + off[1]) * 2 + (half or 0)

    def xz_region(cls, off, half):
        at = pl.ds(pl.multiple_of(source_col(*yz(cls, off)) * SLAB, SLAB), SLAB)
        full = x_full if cls == 0 else z_full
        if half is WHOLE:
            return full.at[:, at, :]
        return full.at[pl.ds(half * (OWNED // 2), OWNED // 2), at, :]

    def u_region(cls, off, half):
        oy, oz = yz(cls, off)
        buf = u_bufs[oy * SIDE + oz]
        if half is WHOLE:
            return buf.at[:, pl.ds(cls * CLASS_ROWS, CLASS_ROWS), :]
        return buf.at[:, pl.ds(cls * CLASS_ROWS + half * HALF_ROWS, HALF_ROWS), :]

    class Tree:
        def __init__(self, region, send_sems, recv_sems, same_place):
            self.region, self.send_sems, self.recv_sems = region, send_sems, recv_sems
            self.same_place, self.sent = same_place, []

        def copy(self, cls, off, dim, sign, half, source=None):
            there = moved(off, dim, sign)
            at = sem_at(cls, there, half)
            here = self.region(cls, off, half)
            copy = pltpu.make_async_remote_copy(
                src_ref=here if source is None else source,
                dst_ref=here if self.same_place else self.region(cls, there, half),
                send_sem=self.send_sems.at[at],
                recv_sem=self.recv_sems.at[at],
                device_id=neighbour(cls, dim, sign),
            )
            copy.start()
            self.sent.append(copy)

        def arrived(self, cls, off, half=WHOLE):
            at = sem_at(cls, off, half)
            here = self.region(cls, off, half)
            pltpu.make_async_remote_copy(
                src_ref=here, dst_ref=here,
                send_sem=self.send_sems.at[at], recv_sem=self.recv_sems.at[at],
                device_id=neighbour(cls, 0, 1),
            ).wait_recv()

        def first(self, sources=(None, None)):
            for dim in (0, 1):
                for sign in (1, -1):
                    for cls in (0, 1):
                        self.copy(cls, (0, 0), dim, sign, WHOLE, sources[cls])

        def near(self):
            for sign, off in ((1, 1), (-1, 3)):
                for cls in (0, 1):
                    self.arrived(cls, (off, 0))
                    self.copy(cls, (off, 0), 0, sign, 0 if sign > 0 else 1)
            for off in (1, 3):
                for cls in (0, 1):
                    for sign in (1, -1):
                        self.copy(cls, (off, 0), 1, sign, WHOLE)
            self.onward(0)

        def onward(self, unit):
            for sign, off in ((1, 1), (-1, 3)):
                for cls in (0, 1):
                    self.arrived(cls, (unit, off))
                    self.copy(cls, (unit, off), 1, sign, 0 if sign > 0 else 1)

        def opposite(self):
            for cls in (0, 1):
                for half in (0, 1):
                    self.arrived(cls, (2, 0), half)
                for sign in (1, -1):
                    self.copy(cls, (2, 0), 1, sign, WHOLE)

        def last(self, unit):
            for cls in (0, 1):
                for half in (0, 1):
                    self.arrived(cls, (unit, 2), half)

        def drain(self):
            for copy in self.sent:
                copy.wait_send()

    xz = Tree(xz_region, xz_send, xz_recv, True)
    ut = Tree(u_region, u_send, u_recv, False)

    lane = lax.broadcasted_iota(i32, (1, C), 1)
    slots = [slot_ref[g] for g in range(GROUPS)]
    blocks = [lax.div(s, GMAX) for s in slots]
    owners = [lax.div(b, OWNED) for b in blocks]
    targets = []
    for g in range(GROUPS):
        earlier = sum([(owners[h] == owners[g]).astype(i32) for h in range(g)], jnp.int32(0))
        targets.append(owners[g] * PAIR + earlier)
    for r in range(ROWS):
        note = jnp.zeros((1, C), i32)
        send_meta[r] = jnp.zeros((8, C), i32)
        for j in range(PAIR):
            t = r * PAIR + j
            src, code = jnp.int32(0), jnp.int32(0)
            for g in range(GROUPS):
                hit = targets[g] == t
                src = jnp.where(hit, g, src)
                code = jnp.where(hit, blocks[g] - owners[g] * OWNED + 1, code)
            note = jnp.where(lane == j, code, note)
            send_ut[t] = basis_ref[src].T
            rows = jnp.zeros((1, C), i32)
            for g in range(GROUPS):
                rows = jnp.where(jnp.full((1, C), targets[g]) == t, rows_ref[pl.ds(g, 1), :], rows)
            send_meta[r, pl.ds(j, 1), :] = rows
        send_meta[r, pl.ds(PAIR, 1), :] = note
    mine = pl.ds(pl.multiple_of(my_col * SLAB, SLAB), SLAB)
    x_full[:, mine, :] = x_ref[...]
    z_full[:, mine, :] = z_ref[...]
    for j in range(PAIR):
        got_ut[my_row * PAIR + j] = send_ut[my_row * PAIR + j]
    got_meta[my_row] = send_meta[my_row]

    pl.semaphore_wait(barrier, ROWS - 1 + COLS - 1)
    xz.first((x_ref, z_ref))

    def part(ref, r):
        many = ref.shape[0] // ROWS
        return ref.at[pl.ds(r * many, many)]

    def exchange(d, r, source, dest, sends, recvs):
        return pltpu.make_async_remote_copy(
            src_ref=part(source, r), dst_ref=part(dest, my_row),
            send_sem=sends.at[d], recv_sem=recvs.at[d], device_id={"row": r},
        )

    def from_row(d, dest, sends, recvs):
        r = lax.rem(my_row + ROWS - d, ROWS)
        return pltpu.make_async_remote_copy(
            src_ref=part(dest, r), dst_ref=part(dest, r),
            send_sem=sends.at[d], recv_sem=recvs.at[d], device_id={"row": r},
        )

    a_sent, m_sent, b_sent = [], [], []
    for d, r in zip(range(1, ROWS), row_peers):
        m_sent.append(exchange(d, r, send_meta, got_meta, m_send, m_recv))
        m_sent[-1].start()
    for d, r in zip(range(1, ROWS), row_peers):
        a_sent.append(exchange(d, r, send_ut, got_ut, a_send, a_recv))
        a_sent[-1].start()

    for d in range(1, ROWS):
        from_row(d, got_meta, m_send, m_recv).wait_recv()
    note_copy = pltpu.make_async_copy(got_meta, small_got, local.at[0])
    note_copy.start()
    note_copy.wait()
    codes = [small_got[t // PAIR, PAIR, t % PAIR] for t in range(ROWS * PAIR)]
    picks = [jnp.int32(0)] * GROUPS
    kept = [jnp.int32(0)] * GROUPS
    count = jnp.int32(0)
    for t in range(ROWS * PAIR):
        for k in range(GROUPS):
            hit = (codes[t] > 0) & (count == k)
            picks[k] = jnp.where(hit, t, picks[k])
            kept[k] = jnp.where(hit, codes[t] - 1, kept[k])
        count = count + (codes[t] > 0).astype(i32)
    table = jnp.full((1, C), 16, i32)
    for k in range(GROUPS):
        table = jnp.where(lane == kept[k], k, table)
    for k in range(GROUPS):
        table = jnp.where(lane == GMAX + k, kept[k], table)
        block_ref[k] = kept[k]
    all_meta[my_col] = jnp.zeros((GMAX, C), i32)
    for k in range(GROUPS):
        rows = jnp.zeros((1, C), i32)
        for t in range(ROWS * PAIR):
            rows = jnp.where(jnp.full((1, C), picks[k]) == t, got_meta[t // PAIR, pl.ds(t % PAIR, 1), :], rows)
        all_meta[my_col, pl.ds(k, 1), :] = rows
    all_meta[my_col, pl.ds(GROUPS, 1), :] = table

    xz.near()

    for d, c in zip(range(1, COLS), col_peers):
        b_sent.append(
            pltpu.make_async_remote_copy(
                src_ref=all_meta.at[my_col], dst_ref=all_meta.at[my_col],
                send_sem=b_send.at[d], recv_sem=b_recv.at[d], device_id={"col": c},
            )
        )
        b_sent[-1].start()

    xz.opposite()
    xz.onward(1)
    xz.onward(3)

    for d in range(1, ROWS):
        from_row(d, got_ut, a_send, a_recv).wait_recv()
    own = u_bufs[0]
    for k in range(GROUPS):
        own[k] = got_ut[picks[k]]

    xz.onward(2)
    ut.first()

    down = lax.broadcasted_iota(i32, (N, C), 0)
    for k in range(GROUPS):
        q_all[k, :, :C] = own[k].T
        q_all[k, :, C:] = jnp.where(down == all_meta[my_col, pl.ds(k, 1), :], 1.0, 0.0).astype(bf16)

    for unit in range(SIDE):
        xz.last(unit)
    for d in range(1, COLS):
        c = lax.rem(my_col + COLS - d, COLS)
        pltpu.make_async_remote_copy(
            src_ref=all_meta.at[c], dst_ref=all_meta.at[c],
            send_sem=b_send.at[d], recv_sem=b_recv.at[d], device_id={"col": c},
        ).wait_recv()
    table_copy = pltpu.make_async_copy(all_meta.at[:, pl.ds(8, 8), :], small_all, local.at[1])
    table_copy.start()
    table_copy.wait()

    def compute(batch):
        cols = [source_col(*off) for off in batch]
        bufs = [u_bufs[oy * SIDE + oz] for oy, oz in batch]

        def step(i, carry):
            for j in range(UNROLL):
                k = i * UNROLL + j
                b = small_all[my_col, GROUPS - 8, GMAX + k]
                codes = [small_all[c, GROUPS - 8, b] for c in cols]
                at = [jnp.where(code < GROUPS, code, 0) for code in codes]
                parts = [
                    (buf[s], row_at(all_meta[c], s))
                    for buf, c, s in zip(bufs, cols, at)
                ]
                for c, code, tile in zip(cols, codes, tiles_of(parts, x_full[b], z_full[b], q_all[k])):
                    tiles_ref[k, pl.ds(pl.multiple_of(c * C, C), C), :] = jnp.where(
                        jnp.full((C, C), code) < GROUPS, tile, 0.0
                    )
            return carry

        lax.fori_loop(0, GROUPS // UNROLL, step, 0)

    ut.near()
    compute(BATCHES[0])
    ut.opposite()
    ut.onward(1)
    ut.last(0)
    compute(BATCHES[1])
    ut.onward(3)
    compute(BATCHES[2])
    ut.onward(2)
    ut.last(1)
    compute(BATCHES[3])
    ut.last(3)
    ut.last(2)
    compute(BATCHES[4])

    xz.drain()
    ut.drain()
    for copy in a_sent + m_sent + b_sent:
        copy.wait_send()


def place_kernel(block_ref, tiles_ref, out_ref, zeros, full_sem, zero_sem):
    zeros[...] = jnp.zeros_like(zeros)
    full = [
        pltpu.make_async_copy(tiles_ref.at[k], out_ref.at[block_ref[k]], full_sem.at[k])
        for k in range(GROUPS)
    ]
    for copy in full:
        copy.start()
    count = jnp.int32(0)
    absent = [jnp.int32(0)] * (OWNED - GROUPS)
    for b in range(OWNED):
        found = block_ref[0] == b
        for k in range(1, GROUPS):
            found = found | (block_ref[k] == b)
        for m in range(OWNED - GROUPS):
            absent[m] = jnp.where(jnp.logical_not(found) & (count == m), b, absent[m])
        count = count + jnp.where(found, 0, 1)
    empty = [
        pltpu.make_async_copy(zeros, out_ref.at[absent[m]], zero_sem.at[m])
        for m in range(OWNED - GROUPS)
    ]
    for copy in empty:
        copy.start()
    for copy in full + empty:
        copy.wait()


def body(basis, row_index, group_slot, x_blocks, zinv_blocks):
    vmem, smem, anywhere = (
        pl.BlockSpec(memory_space=pltpu.VMEM),
        pl.BlockSpec(memory_space=pltpu.SMEM),
        pl.BlockSpec(memory_space=pl.ANY),
    )
    dma = pltpu.SemaphoreType.DMA
    tiles, blocks = pl.pallas_call(
        gather_kernel,
        out_shape=(
            pltpu.VMEM((GROUPS, GMAX * C, C), f32),
            jax.ShapeDtypeStruct((GMAX,), i32),
        ),
        in_specs=[smem, vmem, vmem, vmem, vmem],
        out_specs=(vmem, smem),
        scratch_shapes=[
            pltpu.VMEM((ROWS * PAIR, C, N), bf16),
            pltpu.VMEM((ROWS * PAIR, C, N), bf16),
            pltpu.VMEM((ROWS, 8, C), i32),
            pltpu.VMEM((ROWS, 8, C), i32),
            pltpu.VMEM((COLS, GMAX, C), i32),
            pltpu.SMEM((ROWS, 8, C), i32),
            pltpu.SMEM((COLS, 8, C), i32),
            pltpu.VMEM((OWNED, N, N), bf16),
            pltpu.VMEM((OWNED, N, N), bf16),
            pltpu.VMEM((GROUPS, N, N), bf16),
        ]
        + [pltpu.VMEM((GROUPS, C, N), bf16)] * 16
        + [dma((64,))] * 4
        + [dma((ROWS,))] * 4
        + [dma((COLS,))] * 2
        + [dma((2,))],
        compiler_params=pltpu.CompilerParams(
            collective_id=0, has_side_effects=True, vmem_limit_bytes=44 << 20
        ),
        name="gather_tiles",
    )(group_slot, basis, row_index, x_blocks, zinv_blocks)
    return pl.pallas_call(
        place_kernel,
        out_shape=jax.ShapeDtypeStruct((OWNED, GMAX * C, C), f32),
        in_specs=[smem, vmem],
        out_specs=anywhere,
        scratch_shapes=[pltpu.VMEM((GMAX * C, C), f32), dma((GROUPS,)), dma((OWNED - GROUPS,))],
        compiler_params=pltpu.CompilerParams(vmem_limit_bytes=16 << 20),
        name="place_tiles",
    )(blocks, tiles)


def solution(mesh):
    placed = (
        P(("row", "col"), None, None),
        P(("row", "col"), None),
        P(("row", "col")),
        P("row", "col", None),
        P("row", "col", None),
    )
    return jax.shard_map(
        body, mesh=mesh, in_specs=placed, out_specs=P("row", None, "col"), check_vma=False
    )
```

time: 413 us -> 96.8 us (0.23)
  matrix products: 126 us -> 0 us
  Pallas kernels: 0 us -> 92.3 us
  waiting for transfers between devices: 78.9 us -> 0 us
  other arithmetic: 76.2 us -> 0 us
  local copies, waits for them, and re-layouts: 53.5 us -> 4.2 us
  blocking collectives: 45.6 us -> 0 us
  between operations: 13.5 us -> 0.01 us
  starting transfers between devices: 9.77 us -> 0 us
  loops' own time: 7.33 us -> 0 us
    dot_general x55 -> x0, matrix products: 126 us -> none  [the longest x12 43 us: pair_tiles(): jnp.einsum('pcn,snk->pcsk', images, near_basis, preferred_element_type=jn...]
    pallas_call x0 -> x2, Pallas kernels: none -> 92.3 us  [the longest x1 87.1 us: body(): pl.pallas_call(gather_kernel, out_shape=(pltpu.VMEM((GROUPS, GMAX * C, C)...]
    all_gather x2 -> x0, waiting for transfers between devices: 64 us -> none  [the longest x1 64 us: body(): lax.all_gather(near_basis, 'col', axis=1, tiled=True)]
    mul x12 -> x0, other arithmetic: 52.3 us -> none  [pair_tiles(): tile_sum = tile_sum * row_mask[:, None, None] * column_mask[None, None, :]]
    all_gather x2 -> x0, blocking collectives: 45.6 us -> none  [the longest x1 25.5 us: body(): lax.all_gather(near_rows, 'col', axis=1, tiled=True)]
    squeeze x24 -> x0, local copies, waits for them, and re-layouts: 22.5 us -> none  [the longest x12 20.8 us: body(): lax.map(pair_tiles, (stacked, x_full, z_full, rows_all, mask_all, near_ba...]
    another operation x1 -> x0, other arithmetic: 20.5 us -> none  [body(): stacked = jnp.stack([all_x, all_z], axis=2)]
    all_to_all x2 -> x0, waiting for transfers between devices: 14.8 us -> none  [the longest x1 14.3 us: body(): lax.all_to_all(send_basis, 'row', split_axis=0, concat_axis=0, tiled=True)]
  transfers between devices with their start and end apart: 4 -> 0, of which waited for: 3 -> 0; matrix products, arithmetic and copies ran while one was open for 3% -> 0% of each run, Pallas kernels for 0% -> 0%
where the time goes in v1:
time: 96.8 us; the launch traced here: 96.5 us
  Pallas kernels  92.3 us (95%)
  local copies, waits for them, and re-layouts  4.2 us (4%)
    pallas_call x1, Pallas kernels, body(): pl.pallas_call(gather_kernel, out_shape=(pltpu.VMEM((GROUPS, GMAX * C, C)...  87.1 us
    pallas_call x1, Pallas kernels, body(): pl.pallas_call(place_kernel, out_shape=jax.ShapeDtypeStruct((OWNED, GMAX...  5.21 us
    unnamed x10, local copies, waits for them, and re-layouts  4.2 us

profile of v1, /device:TPU:2, one launch (start us, length us, event | category | flops | bytes accessed | tf_op | source)
XLA Modules:
  0.0 96.5 jit_solution(7492481593793118235)
XLA Ops:
  0.0 0.0 copy-start
  0.0 1.1 %copy-done = bf16[9,256,128]{2,1,0:T(8,128)(2,1)S(1)} copy-done((bf16[9,256,128]{2,1,0:T(8,128)(2,1)S(1)}, bf16[9,256,128]{2,1,0:T(8,128)(2,1)}, u32[]{:S(2)}) %copy-start) | copy-done | bytes 589848
  1.1 0.0 copy-start.1
  1.1 0.9 copy-done.1
  2.0 0.0 copy-start.2
  2.0 0.9 copy-done.2
  2.9 0.0 copy-start.3
  2.9 0.7 copy-done.3
  3.5 0.0 copy-start.4
  3.6 0.7 copy-done.4
  4.2 87.1 %gather_tiles.1 = (f32[9,2048,128]{2,1,0:T(8,128)S(1)}, s32[16]{0:T(128)S(1)}) custom-call(s32[9]{0:T(128)S(1)} %copy-done.4, bf16[9,256,128]{2,1,0:T(8,128)(2,1)S(1)} %copy-done, s32[9,128]{1,0:T(8,128)S(1)} %copy-done.3, bf16[12,16,256]{2,1,0:T(8,128)(2,1)S(1)} %copy-done.1, bf16[12,16,256]{2,1,0:T(8,128)(2,1)S(1)} %copy-done.2), custom_call_target="tpu_custom_call" | custom-call | tf_op jit(solution)/shard_map/gather_tiles/pallas_call | solution.py:386
  91.3 5.2 %place_tiles.1 = f32[12,2048,128]{2,1,0:T(8,128)} custom-call(s32[16]{0:T(128)S(1)} %get-tuple-element.7.block_ref, f32[9,2048,128]{2,1,0:T(8,128)S(1)} %get-tuple-element.8.tiles_ref), custom_call_target="tpu_custom_call" | custom-call | tf_op jit(solution)/shard_map/place_tiles/pallas_call | solution.py:416
Async XLA Ops:
  0.0 1.1 %copy-start = (bf16[9,256,128]{2,1,0:T(8,128)(2,1)S(1)}, bf16[9,256,128]{2,1,0:T(8,128)(2,1)}, u32[]{:S(2)}) copy-start(bf16[9,256,128]{2,1,0:T(8,128)(2,1)} %basis_ref.1) | copy-start | bytes 1769476
  1.1 0.9 copy-start.1
  2.0 0.9 copy-start.2
  2.9 0.7 copy-start.3
  3.5 0.7 copy-start.4

commit v2 on v1

--- a/solution.py
+++ b/solution.py
@@ -15,10 +15,12 @@
 WHOLE = None
 BATCHES = (
     ((0, 0), (1, 0), (3, 0), (0, 1)),
-    ((0, 3), (2, 0), (0, 2), (1, 1)),
+    ((0, 3), (1, 1)),
     ((1, 3), (3, 1), (3, 3)),
+    ((2, 0), (0, 2)),
     ((2, 1), (1, 2)),
-    ((2, 3), (3, 2), (2, 2)),
+    ((2, 3), (3, 2)),
+    ((2, 2),),
 )
 UNROLL = 3
 
@@ -55,21 +57,35 @@
 
 
 def gather_kernel(
-    slot_ref, basis_ref, rows_ref, x_ref, z_ref, tiles_ref, block_ref,
-    send_ut, got_ut, send_meta, got_meta, all_meta, small_got, small_all,
+    slot_ref, basis_hbm, rows_hbm, x_ref, z_ref, tiles_ref, block_ref,
+    basis_ref, rows_ref, send_ut, relay, got_ut, send_meta, got_meta, all_meta, small_got, small_all,
     x_full, z_full, q_all, *rest,
 ):
     u_bufs = rest[:16]
     (xz_send, xz_recv, u_send, u_recv, a_send, a_recv, m_send, m_recv, b_send, b_recv, local) = rest[16:]
     my_row, my_col = lax.axis_index("row"), lax.axis_index("col")
     my_y, my_z = lax.rem(my_col, SIDE), my_col // SIDE
+    my_x, my_core = my_row // 2, lax.rem(my_row, 2)
+    mine = pl.ds(pl.multiple_of(my_col * SLAB, SLAB), SLAB)
+    loads = [
+        pltpu.make_async_copy(source, dest, local.at[i])
+        for i, (source, dest) in enumerate((
+            (basis_hbm, basis_ref),
+            (rows_hbm, rows_ref),
+            (x_ref, x_full.at[:, mine, :]),
+            (z_ref, z_full.at[:, mine, :]),
+        ))
+    ]
+    for copy in loads:
+        copy.start()
 
     row_peers = [lax.rem(my_row + d, ROWS) for d in range(1, ROWS)]
-    col_peers = [lax.rem(my_col + d, COLS) for d in range(1, COLS)]
+    y_peers = [col_of(lax.rem(my_y + d, SIDE), my_z) for d in range(1, SIDE)]
+    z_peers = [col_of(my_y, lax.rem(my_z + d, SIDE)) for d in range(1, SIDE)]
     barrier = pltpu.get_barrier_semaphore()
     for r in row_peers:
         pl.semaphore_signal(barrier, inc=1, device_id={"row": r})
-    for c in col_peers:
+    for c in y_peers + z_peers:
         pl.semaphore_signal(barrier, inc=1, device_id={"col": c})
 
     def source_col(oy, oz):
@@ -134,13 +150,17 @@
                 device_id=neighbour(cls, 0, 1),
             ).wait_recv()
 
-        def first(self, sources=(None, None)):
-            for dim in (0, 1):
+        def first(self, sources=(None, None), dims=(0, 1)):
+            for dim in dims:
                 for sign in (1, -1):
                     for cls in (0, 1):
                         self.copy(cls, (0, 0), dim, sign, WHOLE, sources[cls])
 
         def near(self):
+            self.spread()
+            self.onward(0)
+
+        def spread(self):
             for sign, off in ((1, 1), (-1, 3)):
                 for cls in (0, 1):
                     self.arrived(cls, (off, 0))
@@ -149,7 +169,6 @@
                 for cls in (0, 1):
                     for sign in (1, -1):
                         self.copy(cls, (off, 0), 1, sign, WHOLE)
-            self.onward(0)
 
         def onward(self, unit):
             for sign, off in ((1, 1), (-1, 3)):
@@ -184,6 +203,8 @@
     for g in range(GROUPS):
         earlier = sum([(owners[h] == owners[g]).astype(i32) for h in range(g)], jnp.int32(0))
         targets.append(owners[g] * PAIR + earlier)
+    for copy in loads[:2]:
+        copy.wait()
     for r in range(ROWS):
         note = jnp.zeros((1, C), i32)
         send_meta[r] = jnp.zeros((8, C), i32)
@@ -195,50 +216,75 @@
                 src = jnp.where(hit, g, src)
                 code = jnp.where(hit, blocks[g] - owners[g] * OWNED + 1, code)
             note = jnp.where(lane == j, code, note)
-            send_ut[t] = basis_ref[src].T
+            send_ut[r // 2, j, r % 2] = basis_ref[src].T
             rows = jnp.zeros((1, C), i32)
             for g in range(GROUPS):
                 rows = jnp.where(jnp.full((1, C), targets[g]) == t, rows_ref[pl.ds(g, 1), :], rows)
             send_meta[r, pl.ds(j, 1), :] = rows
         send_meta[r, pl.ds(PAIR, 1), :] = note
-    mine = pl.ds(pl.multiple_of(my_col * SLAB, SLAB), SLAB)
-    x_full[:, mine, :] = x_ref[...]
-    z_full[:, mine, :] = z_ref[...]
     for j in range(PAIR):
-        got_ut[my_row * PAIR + j] = send_ut[my_row * PAIR + j]
+        got_ut[my_row * PAIR + j] = send_ut[my_x, j, my_core]
     got_meta[my_row] = send_meta[my_row]
 
-    pl.semaphore_wait(barrier, ROWS - 1 + COLS - 1)
-    xz.first((x_ref, z_ref))
-
-    def part(ref, r):
-        many = ref.shape[0] // ROWS
-        return ref.at[pl.ds(r * many, many)]
-
-    def exchange(d, r, source, dest, sends, recvs):
+    pl.semaphore_wait(barrier, ROWS - 1 + 2 * (SIDE - 1))
+    def exchange(d, r, sends, recvs):
         return pltpu.make_async_remote_copy(
-            src_ref=part(source, r), dst_ref=part(dest, my_row),
+            src_ref=send_meta.at[r], dst_ref=got_meta.at[my_row],
             send_sem=sends.at[d], recv_sem=recvs.at[d], device_id={"row": r},
         )
 
-    def from_row(d, dest, sends, recvs):
+    def from_row(d, sends, recvs):
         r = lax.rem(my_row + ROWS - d, ROWS)
         return pltpu.make_async_remote_copy(
-            src_ref=part(dest, r), dst_ref=part(dest, r),
+            src_ref=got_meta.at[r], dst_ref=got_meta.at[r],
             send_sem=sends.at[d], recv_sem=recvs.at[d], device_id={"row": r},
         )
 
+    sides = [lax.rem(my_x + 1, SIDE), lax.rem(my_x + SIDE - 1, SIDE)]
+    across = lax.rem(my_x + 2, SIDE)
+
+    def to(source, dest, sem, x, core):
+        return pltpu.make_async_remote_copy(
+            src_ref=source, dst_ref=dest, send_sem=a_send.at[sem], recv_sem=a_recv.at[sem],
+            device_id={"row": x * 2 + core},
+        )
+
+    def pair_of(row):
+        return got_ut.at[pl.ds(row * PAIR, PAIR)]
+
     a_sent, m_sent, b_sent = [], [], []
+    for i in range(2):
+        a_sent.append(to(send_ut.at[across, i], relay.at[i], i, sides[i], my_core))
+    for i in range(2):
+        for same in range(2):
+            core = lax.rem(my_core + same, 2)
+            a_sent.append(to(send_ut.at[sides[i], :, core], pair_of(my_row), 2 + i * 2 + same, sides[i], core))
+    other = lax.rem(my_core + 1, 2)
+    a_sent.append(to(send_ut.at[my_x, :, other], pair_of(my_row), 6, my_x, other))
+
+    for copy in a_sent[:2]:
+        copy.start()
     for d, r in zip(range(1, ROWS), row_peers):
-        m_sent.append(exchange(d, r, send_meta, got_meta, m_send, m_recv))
+        m_sent.append(exchange(d, r, m_send, m_recv))
         m_sent[-1].start()
-    for d, r in zip(range(1, ROWS), row_peers):
-        a_sent.append(exchange(d, r, send_ut, got_ut, a_send, a_recv))
-        a_sent[-1].start()
+    xz.first((x_ref, z_ref))
+    for copy in a_sent[2:]:
+        copy.start()
+
+    xz.spread()
+    for i in range(2):
+        to(relay.at[i], relay.at[i], i, sides[i], my_core).wait_recv()
+        origin = sides[1 - i] * 2 + my_core
+        for core in range(2):
+            a_sent.append(
+                to(relay.at[i, core], got_ut.at[origin * PAIR + i], 7 + i * 4 + core * 2 + my_core, sides[i], core)
+            )
+            a_sent[-1].start()
+    xz.onward(0)
 
     for d in range(1, ROWS):
-        from_row(d, got_meta, m_send, m_recv).wait_recv()
-    note_copy = pltpu.make_async_copy(got_meta, small_got, local.at[0])
+        from_row(d, m_send, m_recv).wait_recv()
+    note_copy = pltpu.make_async_copy(got_meta, small_got, local.at[4])
     note_copy.start()
     note_copy.wait()
     codes = [small_got[t // PAIR, PAIR, t % PAIR] for t in range(ROWS * PAIR)]
@@ -265,29 +311,47 @@
         all_meta[my_col, pl.ds(k, 1), :] = rows
     all_meta[my_col, pl.ds(GROUPS, 1), :] = table
 
-    xz.near()
-
-    for d, c in zip(range(1, COLS), col_peers):
-        b_sent.append(
-            pltpu.make_async_remote_copy(
-                src_ref=all_meta.at[my_col], dst_ref=all_meta.at[my_col],
-                send_sem=b_send.at[d], recv_sem=b_recv.at[d], device_id={"col": c},
-            )
+    def noted(at, sem, c):
+        return pltpu.make_async_remote_copy(
+            src_ref=at, dst_ref=at,
+            send_sem=b_send.at[sem], recv_sem=b_recv.at[sem], device_id={"col": c},
         )
+
+    def notes_of(z):
+        return all_meta.at[pl.ds(z * SIDE, SIDE)]
+
+    for d in range(1, SIDE):
+        b_sent.append(noted(all_meta.at[my_col], d, y_peers[d - 1]))
         b_sent[-1].start()
-
     xz.opposite()
+    for d in range(1, SIDE):
+        c = col_of(lax.rem(my_y + SIDE - d, SIDE), my_z)
+        noted(all_meta.at[c], d, c).wait_recv()
+    for d in range(1, SIDE):
+        b_sent.append(noted(notes_of(my_z), SIDE + d, z_peers[d - 1]))
+        b_sent[-1].start()
     xz.onward(1)
     xz.onward(3)
 
-    for d in range(1, ROWS):
-        from_row(d, got_ut, a_send, a_recv).wait_recv()
+    for i in range(2):
+        for same in range(2):
+            core = lax.rem(my_core + same, 2)
+            dest = pair_of(sides[1 - i] * 2 + core)
+            to(dest, dest, 2 + i * 2 + same, sides[i], core).wait_recv()
+    dest = pair_of(my_x * 2 + other)
+    to(dest, dest, 6, my_x, other).wait_recv()
+    for i in range(2):
+        for core in range(2):
+            dest = got_ut.at[(across * 2 + core) * PAIR + i]
+            sem = 7 + i * 4 + my_core * 2 + core
+            to(dest, dest, sem, sides[i], core).wait_recv()
     own = u_bufs[0]
     for k in range(GROUPS):
         own[k] = got_ut[picks[k]]
 
+    ut.first(dims=(0,))
     xz.onward(2)
-    ut.first()
+    ut.first(dims=(1,))
 
     down = lax.broadcasted_iota(i32, (N, C), 0)
     for k in range(GROUPS):
@@ -296,13 +360,12 @@
 
     for unit in range(SIDE):
         xz.last(unit)
-    for d in range(1, COLS):
-        c = lax.rem(my_col + COLS - d, COLS)
-        pltpu.make_async_remote_copy(
-            src_ref=all_meta.at[c], dst_ref=all_meta.at[c],
-            send_sem=b_send.at[d], recv_sem=b_recv.at[d], device_id={"col": c},
-        ).wait_recv()
-    table_copy = pltpu.make_async_copy(all_meta.at[:, pl.ds(8, 8), :], small_all, local.at[1])
+    for copy in loads[2:]:
+        copy.wait()
+    for d in range(1, SIDE):
+        z = lax.rem(my_z + SIDE - d, SIDE)
+        noted(notes_of(z), SIDE + d, col_of(my_y, z)).wait_recv()
+    table_copy = pltpu.make_async_copy(all_meta.at[:, pl.ds(8, 8), :], small_all, local.at[5])
     table_copy.start()
     table_copy.wait()
 
@@ -332,16 +395,18 @@
     compute(BATCHES[0])
     ut.opposite()
     ut.onward(1)
-    ut.last(0)
     compute(BATCHES[1])
     ut.onward(3)
     compute(BATCHES[2])
+    ut.last(0)
+    compute(BATCHES[3])
     ut.onward(2)
     ut.last(1)
-    compute(BATCHES[3])
+    compute(BATCHES[4])
     ut.last(3)
+    compute(BATCHES[5])
     ut.last(2)
-    compute(BATCHES[4])
+    compute(BATCHES[6])
 
     xz.drain()
     ut.drain()
@@ -377,7 +442,8 @@
 
 
 def body(basis, row_index, group_slot, x_blocks, zinv_blocks):
-    vmem, smem, anywhere = (
+    hbm, vmem, smem, anywhere = (
+        pl.BlockSpec(memory_space=pltpu.HBM),
         pl.BlockSpec(memory_space=pltpu.VMEM),
         pl.BlockSpec(memory_space=pltpu.SMEM),
         pl.BlockSpec(memory_space=pl.ANY),
@@ -389,10 +455,13 @@
             pltpu.VMEM((GROUPS, GMAX * C, C), f32),
             jax.ShapeDtypeStruct((GMAX,), i32),
         ),
-        in_specs=[smem, vmem, vmem, vmem, vmem],
+        in_specs=[smem, hbm, hbm, hbm, hbm],
         out_specs=(vmem, smem),
         scratch_shapes=[
-            pltpu.VMEM((ROWS * PAIR, C, N), bf16),
+            pltpu.VMEM((GROUPS, N, C), bf16),
+            pltpu.VMEM((GROUPS, C), i32),
+            pltpu.VMEM((SIDE, PAIR, 2, C, N), bf16),
+            pltpu.VMEM((2, 2, C, N), bf16),
             pltpu.VMEM((ROWS * PAIR, C, N), bf16),
             pltpu.VMEM((ROWS, 8, C), i32),
             pltpu.VMEM((ROWS, 8, C), i32),
@@ -405,11 +474,12 @@
         ]
         + [pltpu.VMEM((GROUPS, C, N), bf16)] * 16
         + [dma((64,))] * 4
-        + [dma((ROWS,))] * 4
-        + [dma((COLS,))] * 2
-        + [dma((2,))],
+        + [dma((16,))] * 2
+        + [dma((ROWS,))] * 2
+        + [dma((2 * SIDE,))] * 2
+        + [dma((6,))],
         compiler_params=pltpu.CompilerParams(
-            collective_id=0, has_side_effects=True, vmem_limit_bytes=44 << 20
+            collective_id=0, has_side_effects=True, vmem_limit_bytes=57_500_000
         ),
         name="gather_tiles",
     )(group_slot, basis, row_index, x_blocks, zinv_blocks)

time: 96.8 us -> 88.8 us (0.917)
  Pallas kernels: 92.3 us -> 87.1 us
  local copies, waits for them, and re-layouts: 4.2 us -> 0.62 us
    pallas_call x1, Pallas kernels: 87.1 us -> 81.9 us  [body(): pl.pallas_call(gather_kernel, out_shape=(pltpu.VMEM((GROUPS, GMAX * C, C)...]
    unnamed x10 -> x2, local copies, waits for them, and re-layouts: 4.2 us -> 0.62 us
where the time goes in v2:
time: 88.8 us; the launch traced here: 87.7 us
  Pallas kernels  87.1 us (98%)
    pallas_call x1, Pallas kernels, body(): pl.pallas_call(gather_kernel, out_shape=(pltpu.VMEM((GROUPS, GMAX * C, C)...  81.9 us
    pallas_call x1, Pallas kernels, body(): pl.pallas_call(place_kernel, out_shape=jax.ShapeDtypeStruct((OWNED, GMAX...  5.2 us

profile of v2, /device:TPU:2, one launch (start us, length us, event | category | flops | bytes accessed | tf_op | source)
XLA Modules:
  0.0 87.7 jit_solution(11670388238185639116)
XLA Ops:
  0.0 81.9 %gather_tiles.1 = (f32[9,2048,128]{2,1,0:T(8,128)S(1)}, s32[16]{0:T(128)}) custom-call(s32[9]{0:T(128)} %slot_ref.1, bf16[9,256,128]{2,1,0:T(8,128)(2,1)} %basis_hbm.1, s32[9,128]{1,0:T(8,128)} %rows_hbm.1, bf16[12,16,256]{2,1,0:T(8,128)(2,1)} %x_ref.1, bf16[12,16,256]{2,1,0:T(8,128)(2,1)} %z_ref.1), custom_call_target="tpu_custom_call" | custom-call | tf_op jit(solution)/shard_map/gather_tiles/pallas_call | solution.py:452
  81.9 0.0 copy-start
  81.9 0.6 copy-done
  82.5 5.2 %place_tiles.1 = f32[12,2048,128]{2,1,0:T(8,128)} custom-call(s32[16]{0:T(128)S(1)} %copy-done, f32[9,2048,128]{2,1,0:T(8,128)S(1)} %get-tuple-element.8.tiles_ref), custom_call_target="tpu_custom_call" | custom-call | tf_op jit(solution)/shard_map/place_tiles/pallas_call | solution.py:486
Async XLA Ops:
  81.9 0.6 copy-start

commit v3 on v2

--- a/solution.py
+++ b/solution.py
@@ -18,10 +18,8 @@
     ((0, 3), (1, 1)),
     ((1, 3), (3, 1), (3, 3)),
     ((2, 0), (0, 2)),
-    ((2, 1), (1, 2)),
-    ((2, 3), (3, 2)),
-    ((2, 2),),
 )
+LATE = ((2, 1), (1, 2), (2, 3), (3, 2), (2, 2))
 UNROLL = 3
 
 
@@ -43,10 +41,7 @@
 
 def tiles_of(parts, x, z, q):
     stack = jnp.concatenate([a for ut, rows in parts for a in (ut, one_hot_rows(rows))], axis=0)
-    sx = jnp.dot(stack, x, preferred_element_type=f32).astype(bf16)
-    sz = jnp.dot(stack, z, preferred_element_type=f32).astype(bf16)
-    tx = jnp.dot(sx, q, preferred_element_type=f32)
-    tz = jnp.dot(sz, q, preferred_element_type=f32)
+    tx, tz = products_of(stack, x, z, q)
     out = []
     for i in range(len(parts)):
         lo, mid, hi = 2 * C * i, 2 * C * i + C, 2 * C * i + 2 * C
@@ -56,10 +51,19 @@
     return out
 
 
+def products_of(stack, x, z, q):
+    sx = jnp.dot(stack, x, preferred_element_type=f32).astype(bf16)
+    sz = jnp.dot(stack, z, preferred_element_type=f32).astype(bf16)
+    return (
+        jnp.dot(sx, q, preferred_element_type=f32),
+        jnp.dot(sz, q, preferred_element_type=f32),
+    )
+
+
 def gather_kernel(
     slot_ref, basis_hbm, rows_hbm, x_ref, z_ref, tiles_ref, block_ref,
     basis_ref, rows_ref, send_ut, relay, got_ut, send_meta, got_meta, all_meta, small_got, small_all,
-    x_full, z_full, q_all, *rest,
+    x_full, z_full, q_all, ahead, *rest,
 ):
     u_bufs = rest[:16]
     (xz_send, xz_recv, u_send, u_recv, a_send, a_recv, m_send, m_recv, b_send, b_recv, local) = rest[16:]
@@ -267,7 +271,9 @@
     for d, r in zip(range(1, ROWS), row_peers):
         m_sent.append(exchange(d, r, m_send, m_recv))
         m_sent[-1].start()
-    xz.first((x_ref, z_ref))
+    for copy in loads[2:]:
+        copy.wait()
+    xz.first()
     for copy in a_sent[2:]:
         copy.start()
 
@@ -360,8 +366,6 @@
 
     for unit in range(SIDE):
         xz.last(unit)
-    for copy in loads[2:]:
-        copy.wait()
     for d in range(1, SIDE):
         z = lax.rem(my_z + SIDE - d, SIDE)
         noted(notes_of(z), SIDE + d, col_of(my_y, z)).wait_recv()
@@ -369,29 +373,69 @@
     table_copy.start()
     table_copy.wait()
 
+    def places(k, cols):
+        b = small_all[my_col, GROUPS - 8, GMAX + k]
+        codes = [small_all[c, GROUPS - 8, b] for c in cols]
+        return b, codes, [jnp.where(code < GROUPS, code, 0) for code in codes]
+
+    def keep(k, c, code, tile):
+        tiles_ref[k, pl.ds(pl.multiple_of(c * C, C), C), :] = jnp.where(
+            jnp.full((C, C), code) < GROUPS, tile, 0.0
+        )
+
+    def per_group(work, unroll=UNROLL):
+        def step(i, carry):
+            for j in range(unroll):
+                work(i * unroll + j)
+            return carry
+
+        lax.fori_loop(0, GROUPS // unroll, step, 0)
+
     def compute(batch):
         cols = [source_col(*off) for off in batch]
         bufs = [u_bufs[oy * SIDE + oz] for oy, oz in batch]
 
-        def step(i, carry):
-            for j in range(UNROLL):
-                k = i * UNROLL + j
-                b = small_all[my_col, GROUPS - 8, GMAX + k]
-                codes = [small_all[c, GROUPS - 8, b] for c in cols]
-                at = [jnp.where(code < GROUPS, code, 0) for code in codes]
-                parts = [
-                    (buf[s], row_at(all_meta[c], s))
-                    for buf, c, s in zip(bufs, cols, at)
-                ]
-                for c, code, tile in zip(cols, codes, tiles_of(parts, x_full[b], z_full[b], q_all[k])):
-                    tiles_ref[k, pl.ds(pl.multiple_of(c * C, C), C), :] = jnp.where(
-                        jnp.full((C, C), code) < GROUPS, tile, 0.0
-                    )
-            return carry
-
-        lax.fori_loop(0, GROUPS // UNROLL, step, 0)
+        def work(k):
+            b, codes, at = places(k, cols)
+            parts = [(buf[s], row_at(all_meta[c], s)) for buf, c, s in zip(bufs, cols, at)]
+            for c, code, tile in zip(cols, codes, tiles_of(parts, x_full[b], z_full[b], q_all[k])):
+                keep(k, c, code, tile)
+
+        per_group(work)
+
+    def compute_ahead():
+        cols = [source_col(*off) for off in LATE]
+
+        def work(k):
+            b, _, at = places(k, cols)
+            stack = jnp.concatenate(
+                [one_hot_rows(row_at(all_meta[c], s)) for c, s in zip(cols, at)], axis=0
+            )
+            tx, tz = products_of(stack, x_full[b], z_full[b], q_all[k])
+            for i in range(len(LATE)):
+                ahead[k, i, :, :N] = tx[i * C : i * C + C]
+                ahead[k, i, :, N:] = tz[i * C : i * C + C]
+
+        per_group(work)
+
+    def compute_late(first, last):
+        cols = [source_col(*off) for off in LATE[first:last]]
+        bufs = [u_bufs[oy * SIDE + oz] for oy, oz in LATE[first:last]]
+
+        def work(k):
+            b, codes, at = places(k, cols)
+            stack = jnp.concatenate([buf[s] for buf, s in zip(bufs, at)], axis=0)
+            tx, tz = products_of(stack, x_full[b], z_full[b], q_all[k])
+            for i, (c, code) in enumerate(zip(cols, codes)):
+                su0, se0 = tx[i * C : i * C + C, :C], tx[i * C : i * C + C, C:]
+                su2, se2 = tz[i * C : i * C + C, :C], tz[i * C : i * C + C, C:]
+                su1, se1, su3, se3 = [ahead[k, first + i, :, m * C : m * C + C] for m in range(4)]
+                keep(k, c, code, su1 * se2 + se1 * su2 + su0 * se3 + se0 * su3)
+
+        per_group(work, GROUPS)
 
     ut.near()
+    compute_ahead()
     compute(BATCHES[0])
     ut.opposite()
     ut.onward(1)
@@ -402,11 +446,11 @@
     compute(BATCHES[3])
     ut.onward(2)
     ut.last(1)
-    compute(BATCHES[4])
+    compute_late(0, 2)
     ut.last(3)
-    compute(BATCHES[5])
+    compute_late(2, 4)
     ut.last(2)
-    compute(BATCHES[6])
+    compute_late(4, 5)
 
     xz.drain()
     ut.drain()
@@ -471,6 +515,7 @@
             pltpu.VMEM((OWNED, N, N), bf16),
             pltpu.VMEM((OWNED, N, N), bf16),
             pltpu.VMEM((GROUPS, N, N), bf16),
+            pltpu.VMEM((GROUPS, len(LATE), C, 2 * N), f32),
         ]
         + [pltpu.VMEM((GROUPS, C, N), bf16)] * 16
         + [dma((64,))] * 4

time: 88.8 us -> 86.8 us (0.977)
  Pallas kernels: 87.1 us -> 84.9 us
    pallas_call x1, Pallas kernels: 81.9 us -> 79.7 us  [body(): pl.pallas_call(gather_kernel, out_shape=(pltpu.VMEM((GROUPS, GMAX * C, C)...]
where the time goes in v3:
time: 86.8 us; the launch traced here: 85.6 us
  Pallas kernels  84.9 us (98%)
    pallas_call x1, Pallas kernels, body(): pl.pallas_call(gather_kernel, out_shape=(pltpu.VMEM((GROUPS, GMAX * C, C)...  79.7 us
    pallas_call x1, Pallas kernels, body(): pl.pallas_call(place_kernel, out_shape=jax.ShapeDtypeStruct((OWNED, GMAX...  5.2 us

profile of v3, /device:TPU:2, one launch (start us, length us, event | category | flops | bytes accessed | tf_op | source)
XLA Modules:
  0.0 85.6 jit_solution(1506874789405961278)
XLA Ops:
  0.0 79.7 %gather_tiles.1 = (f32[9,2048,128]{2,1,0:T(8,128)S(1)}, s32[16]{0:T(128)}) custom-call(s32[9]{0:T(128)} %slot_ref.1, bf16[9,256,128]{2,1,0:T(8,128)(2,1)} %basis_hbm.1, s32[9,128]{1,0:T(8,128)} %rows_hbm.1, bf16[12,16,256]{2,1,0:T(8,128)(2,1)} %x_ref.1, bf16[12,16,256]{2,1,0:T(8,128)(2,1)} %z_ref.1), custom_call_target="tpu_custom_call" | custom-call | tf_op jit(solution)/shard_map/gather_tiles/pallas_call | solution.py:496
  79.7 0.0 copy-start
  79.7 0.6 copy-done
  80.4 5.2 %place_tiles.1 = f32[12,2048,128]{2,1,0:T(8,128)} custom-call(s32[16]{0:T(128)S(1)} %copy-done, f32[9,2048,128]{2,1,0:T(8,128)S(1)} %get-tuple-element.8.tiles_ref), custom_call_target="tpu_custom_call" | custom-call | tf_op jit(solution)/shard_map/place_tiles/pallas_call | solution.py:531
Async XLA Ops:
  79.7 0.6 copy-start

commit v4 on v3

--- a/solution.py
+++ b/solution.py
@@ -308,7 +308,7 @@
         table = jnp.where(lane == kept[k], k, table)
     for k in range(GROUPS):
         table = jnp.where(lane == GMAX + k, kept[k], table)
-        block_ref[k] = kept[k]
+    block_ref[...] = jnp.broadcast_to(table, block_ref.shape)
     all_meta[my_col] = jnp.zeros((GMAX, C), i32)
     for k in range(GROUPS):
         rows = jnp.zeros((1, C), i32)
@@ -458,8 +458,12 @@
         copy.wait_send()
 
 
-def place_kernel(block_ref, tiles_ref, out_ref, zeros, full_sem, zero_sem):
+def place_kernel(table_ref, tiles_ref, out_ref, zeros, table, full_sem, zero_sem, table_sem):
+    table_copy = pltpu.make_async_copy(table_ref, table, table_sem)
+    table_copy.start()
     zeros[...] = jnp.zeros_like(zeros)
+    table_copy.wait()
+    block_ref = [table[0, GMAX + k] for k in range(GROUPS)]
     full = [
         pltpu.make_async_copy(tiles_ref.at[k], out_ref.at[block_ref[k]], full_sem.at[k])
         for k in range(GROUPS)
@@ -497,10 +501,10 @@
         gather_kernel,
         out_shape=(
             pltpu.VMEM((GROUPS, GMAX * C, C), f32),
-            jax.ShapeDtypeStruct((GMAX,), i32),
+            pltpu.VMEM((8, C), i32),
         ),
         in_specs=[smem, hbm, hbm, hbm, hbm],
-        out_specs=(vmem, smem),
+        out_specs=(vmem, vmem),
         scratch_shapes=[
             pltpu.VMEM((GROUPS, N, C), bf16),
             pltpu.VMEM((GROUPS, C), i32),
@@ -531,9 +535,9 @@
     return pl.pallas_call(
         place_kernel,
         out_shape=jax.ShapeDtypeStruct((OWNED, GMAX * C, C), f32),
-        in_specs=[smem, vmem],
+        in_specs=[vmem, vmem],
         out_specs=anywhere,
-        scratch_shapes=[pltpu.VMEM((GMAX * C, C), f32), dma((GROUPS,)), dma((OWNED - GROUPS,))],
+        scratch_shapes=[pltpu.VMEM((GMAX * C, C), f32), pltpu.SMEM((8, C), i32), dma((GROUPS,)), dma((OWNED - GROUPS,)), dma],
         compiler_params=pltpu.CompilerParams(vmem_limit_bytes=16 << 20),
         name="place_tiles",
     )(blocks, tiles)

time: 86.8 us -> 85.7 us (0.987)
  no operation moved by 1% of the time
where the time goes in v4:
time: 85.7 us; the launch traced here: 84.5 us
  Pallas kernels  84.5 us (99%)
    pallas_call x1, Pallas kernels, body(): pl.pallas_call(gather_kernel, out_shape=(pltpu.VMEM((GROUPS, GMAX * C, C)...  79.2 us
    pallas_call x1, Pallas kernels, body(): pl.pallas_call(place_kernel, out_shape=jax.ShapeDtypeStruct((OWNED, GMAX...  5.28 us

profile of v4, /device:TPU:2, one launch (start us, length us, event | category | flops | bytes accessed | tf_op | source)
XLA Modules:
  0.0 84.5 jit_solution(2078223094071952396)
XLA Ops:
  0.0 79.2 %gather_tiles.1 = (f32[9,2048,128]{2,1,0:T(8,128)S(1)}, s32[8,128]{1,0:T(8,128)S(1)}) custom-call(s32[9]{0:T(128)} %slot_ref.1, bf16[9,256,128]{2,1,0:T(8,128)(2,1)} %basis_hbm.1, s32[9,128]{1,0:T(8,128)} %rows_hbm.1, bf16[12,16,256]{2,1,0:T(8,128)(2,1)} %x_ref.1, bf16[12,16,256]{2,1,0:T(8,128)(2,1)} %z_ref.1), custom_call_target="tpu_custom_call" | custom-call | tf_op jit(solution)/shard_map/gather_tiles/pallas_call | solution.py:500
  79.2 5.3 %place_tiles.1 = f32[12,2048,128]{2,1,0:T(8,128)} custom-call(s32[8,128]{1,0:T(8,128)S(1)} %get-tuple-element.7.table_ref, f32[9,2048,128]{2,1,0:T(8,128)S(1)} %get-tuple-element.8.tiles_ref), custom_call_target="tpu_custom_call" | custom-call | tf_op jit(solution)/shard_map/place_tiles/pallas_call | solution.py:535
